TPU v7x, 32 devices: a whole 2x2x4 slice. The times are simulated.
32 devices in a mesh: dp: 4 (over z), expert: 2 (over x), tensor: 4 (over y, core).
Axes of the slice: x: 2, y: 2, z: 4, core: 2. Of those that a mesh axis runs over, the one named last changes fastest.
Arguments:
- tokens: bfloat16 [256, 4096], P(('dp', 'expert', 'tensor')), may hold values from -6 to 6
- out_grad: bfloat16 [256, 4096], P(('dp', 'expert', 'tensor')), may hold values from -4 to 4
- route_probs: float32 [256, 2], P(('dp', 'expert')), may hold values from 0.2 to 1
- expert_ids: int32 [256, 2], P(('dp', 'expert')), may hold values from 0 to 7, as said below
- slot_index: int32 [256, 2], P(('dp', 'expert')), may hold values from 0 to 10, as said below
- w_gate: bfloat16 [8, 4096, 7168], P('expert', 'dp', 'tensor'), may hold values from -0.09375 to 0.09375
- w_up: bfloat16 [8, 4096, 7168], P('expert', 'dp', 'tensor'), may hold values from -0.09375 to 0.09375
- w_down: bfloat16 [8, 7168, 4096], P('expert', 'tensor', 'dp'), may hold values from -0.0625 to 0.0625
Outputs:
- token_grad: bfloat16 [256, 4096], P(('dp', 'expert', 'tensor'))
- grad_gate: bfloat16 [8, 4096, 7168], P('expert', 'dp', 'tensor')
- grad_up: bfloat16 [8, 4096, 7168], P('expert', 'dp', 'tensor')
- grad_down: bfloat16 [8, 7168, 4096], P('expert', 'tensor', 'dp')
Inputs may be any that keep to these rules, and one draw needn't show every extreme that they name: `expert_ids`: the 2 entries of a token are different experts. slot_index[t, k] counts the earlier routes to expert_ids[t, k] within the token's routing block of 32 rows, in order of tokens and then of routes; the value 10 marks a route past the capacity, which is dropped (a count of 10 or more is given as 10). In every draw some expert is filled to 10 slots in every block.
All inputs are finite; a program needn't handle non-finite values.
Results may differ from a plain program's by a relative error of at most 0.011.
Values may be sent and summed in bfloat16 or wider, within the bound.
A program may use at most 192 MiB of HBM per device.

v0:
```python
import jax
import jax.numpy as jnp
from jax import lax
from jax.sharding import PartitionSpec as P

EXPERTS = 8
TOP = 2


def route_tables(expert_ids, slot_index, capacity):
    target = slot_index * EXPERTS + expert_ids
    target = jnp.where(slot_index < capacity, target, -1)
    places = jnp.arange(capacity * EXPERTS, dtype=jnp.int32)
    return [(places[:, None] == target[None, :, k]).astype(jnp.bfloat16) for k in range(TOP)]


def swiglu_back(pre_gate, pre_up, grad_hidden):
    sigmoid_gate = jax.nn.sigmoid(pre_gate)
    silu_gate = pre_gate * sigmoid_gate
    hidden = (silu_gate * pre_up).astype(jnp.bfloat16)
    up_delta = (grad_hidden * silu_gate).astype(jnp.bfloat16)
    gate_delta = (
        grad_hidden * pre_up * sigmoid_gate * (1.0 + pre_gate * (1.0 - sigmoid_gate))
    ).astype(jnp.bfloat16)
    return (hidden, gate_delta, up_delta)


def shards(tokens, out_grad, route_probs, expert_ids, slot_index, w_gate, w_up, w_down):
    block_x, block_dy = (
        lax.all_gather(tokens, "tensor", axis=0, tiled=True),
        lax.all_gather(out_grad, "tensor", axis=0, tiled=True),
    )
    block_rows = block_x.shape[0]
    model_width = block_x.shape[1]
    capacity = 5 * block_rows * TOP // (4 * EXPERTS)
    tables = route_tables(expert_ids, slot_index, capacity)
    table_sum = tables[0] + tables[1]
    x_buf = jnp.dot(table_sum, block_x, preferred_element_type=jnp.float32).astype(jnp.bfloat16)
    grad_buf = jnp.zeros((capacity * EXPERTS, model_width), jnp.float32)
    for k in range(TOP):
        scaled = (route_probs[:, k : k + 1] * block_dy.astype(jnp.float32)).astype(jnp.bfloat16)
        grad_buf = grad_buf + jnp.dot(tables[k], scaled, preferred_element_type=jnp.float32)
    grad_buf = grad_buf.astype(jnp.bfloat16)
    recv_x, recv_grad = (
        lax.all_to_all(
            lax.all_to_all(
                x_buf.reshape(capacity, EXPERTS, model_width),
                "dp",
                split_axis=2,
                concat_axis=0,
                tiled=True,
            ),
            "expert",
            split_axis=1,
            concat_axis=1,
            tiled=True,
        ),
        lax.all_to_all(
            lax.all_to_all(
                grad_buf.reshape(capacity, EXPERTS, model_width),
                "dp",
                split_axis=2,
                concat_axis=0,
                tiled=True,
            ),
            "expert",
            split_axis=1,
            concat_axis=1,
            tiled=True,
        ),
    )
    local_experts = w_gate.shape[0]
    sources = EXPERTS // local_experts
    rows_all = recv_x.shape[0]
    slice_width = recv_x.shape[2]
    token_rows = recv_x.reshape(rows_all, sources, local_experts, slice_width)
    grad_rows = recv_grad.reshape(rows_all, sources, local_experts, slice_width)
    pre_gate = jnp.einsum("cnld,ldf->cnlf", token_rows, w_gate, preferred_element_type=jnp.float32)
    pre_up = jnp.einsum("cnld,ldf->cnlf", token_rows, w_up, preferred_element_type=jnp.float32)
    grad_hidden = jnp.einsum(
        "cnld,lfd->cnlf", grad_rows, w_down, preferred_element_type=jnp.float32
    )
    partial_terms = lax.psum(jnp.stack([pre_gate, pre_up, grad_hidden], 3), "dp")
    hidden, gate_delta, up_delta = swiglu_back(
        partial_terms[:, :, :, 0], partial_terms[:, :, :, 1], partial_terms[:, :, :, 2]
    )
    grad_down = jnp.einsum(
        "cnlf,cnld->lfd", hidden, grad_rows, preferred_element_type=jnp.float32
    ).astype(jnp.bfloat16)
    grad_gate = jnp.einsum(
        "cnld,cnlf->ldf", token_rows, gate_delta, preferred_element_type=jnp.float32
    ).astype(jnp.bfloat16)
    grad_up = jnp.einsum(
        "cnld,cnlf->ldf", token_rows, up_delta, preferred_element_type=jnp.float32
    ).astype(jnp.bfloat16)
    row_grad = jnp.einsum("cnlf,ldf->cnld", gate_delta, w_gate, preferred_element_type=jnp.float32)
    row_grad = row_grad + jnp.einsum(
        "cnlf,ldf->cnld", up_delta, w_up, preferred_element_type=jnp.float32
    )
    table_float = table_sum.astype(jnp.float32)
    back_rows = lax.all_to_all(
        lax.all_to_all(
            row_grad.reshape(rows_all, EXPERTS, slice_width),
            "dp",
            split_axis=0,
            concat_axis=2,
            tiled=True,
        ),
        "expert",
        split_axis=1,
        concat_axis=1,
        tiled=True,
    )
    token_part = jnp.dot(
        table_float.T,
        back_rows.reshape(capacity * EXPERTS, model_width),
        precision=lax.Precision.HIGHEST,
        preferred_element_type=jnp.float32,
    )
    token_grad = lax.psum_scatter(token_part, "tensor", scatter_dimension=0, tiled=True)
    return (token_grad.astype(jnp.bfloat16), grad_gate, grad_up, grad_down)


def solution(mesh):
    placed = (
        P(("dp", "expert", "tensor"), None),
        P(("dp", "expert", "tensor"), None),
        P(("dp", "expert"), None),
        P(("dp", "expert"), None),
        P(("dp", "expert"), None),
        P("expert", "dp", "tensor"),
        P("expert", "dp", "tensor"),
        P("expert", "tensor", "dp"),
    )
    return jax.shard_map(
        shards,
        mesh=mesh,
        in_specs=placed,
        out_specs=(
            P(("dp", "expert", "tensor"), None),
            P("expert", "dp", "tensor"),
            P("expert", "dp", "tensor"),
            P("expert", "tensor", "dp"),
        ),
        check_vma=False,
    )
```

profile of v0, /device:TPU:0, one launch (start us, length us, event | category | flops | bytes accessed | tf_op | source)
XLA Modules:
  0.0 552.5 jit_solution(11450210532100585577)
XLA Ops:
  7.9 7.4 %all_gather.6 = bf16[32,4096]{1,0:T(8,128)(2,1)S(1)} all-gather(bf16[8,4096]{1,0:T(8,128)(2,1)} %param.8), channel_id=1, replica_groups=mesh['dp'=4,'expert'=2,'tensor'=4] {'tensor'}, dimensions={0}, use_global_device_ids=true | all-gather | bytes 327680 | tf_op jit(solution)/shard_map/all_gather | solution.py:30
  15.6 7.5 %copy.72 = bf16[10,8,4096]{0,1,2:T(8,128)(2,1)} copy(bf16[10,8,4096]{2,1,0:T(8,128)(2,1)S(1)} %fusion.11) | data formatting | bytes 1310720 | tf_op jit(solution)/shard_map/reshape | solution.py:47
  23.1 18.2 %reshape.43 = bf16[4,2,40960]{2,1,0:T(2,128)(2,1)} reshape(bf16[4096,8,10]{2,1,0:T(8,128)(2,1)} %bitcast.112) | data formatting | bytes 1310720
  41.3 4.9 all-to-all-start
  46.2 5.8 %all_gather.7 = bf16[32,4096]{1,0:T(8,128)(2,1)S(1)} all-gather(bf16[8,4096]{1,0:T(8,128)(2,1)S(1)} %copy-done.1), channel_id=1, replica_groups=mesh['dp'=4,'expert'=2,'tensor'=4] {'tensor'}, dimensions={0}, use_global_device_ids=true | all-gather | bytes 327680 | tf_op jit(solution)/shard_map/all_gather | solution.py:31
  52.8 7.5 %copy.78 = bf16[10,8,4096]{0,1,2:T(8,128)(2,1)} copy(bf16[10,8,4096]{2,1,0:T(8,128)(2,1)S(1)} %fusion.12) | data formatting | bytes 1310720 | tf_op jit(solution)/shard_map/reshape | solution.py:60
  60.2 18.2 %reshape.41 = bf16[4,2,40960]{2,1,0:T(2,128)(2,1)} reshape(bf16[4096,8,10]{2,1,0:T(8,128)(2,1)} %bitcast.113) | data formatting | bytes 1310720
  78.4 5.6 %all-to-all-start.2 = ((bf16[4,2,40960]{2,1,0:T(2,128)(2,1)}), bf16[4,2,40960]{2,1,0:T(2,128)(2,1)S(1)}, u32[]{:S(2)}, u32[]{:S(2)}) async-start(bf16[4,2,40960]{2,1,0:T(2,128)(2,1)} %reshape.41), calls=%async_computation.2 | async-start | bytes 1310720 | tf_op jit(solution)/shard_map/all_to_all | solution.py:59
  84.0 19.8 %reshape.44 = bf16[4096,8,10]{2,1,0:T(8,128)(2,1)} reshape(bf16[4,2,40960]{2,1,0:T(2,128)(2,1)S(1)} %all-to-all-done) | data formatting | bytes 1310720
  103.8 9.1 %copy.95 = bf16[10,8,4,1024]{3,2,1,0:T(4,128)(2,1)S(1)} copy(bf16[10,8,4,1024]{0,1,3,2:T(8,128)(2,1)} %bitcast.114) | data formatting | bytes 1310720 | tf_op jit(solution)/shard_map/all_to_all | solution.py:46
  114.3 3.5 all-to-all-start.1
  117.8 19.8 %reshape.42 = bf16[4096,8,10]{2,1,0:T(8,128)(2,1)} reshape(bf16[4,2,40960]{2,1,0:T(2,128)(2,1)S(1)} %all-to-all-done.2) | data formatting | bytes 1310720
  137.6 9.1 %copy.96 = bf16[10,8,4,1024]{3,2,1,0:T(4,128)(2,1)S(1)} copy(bf16[10,8,4,1024]{0,1,3,2:T(8,128)(2,1)} %bitcast.115) | data formatting | bytes 1310720 | tf_op jit(solution)/shard_map/all_to_all | solution.py:59
  148.1 4.3 all-to-all-start.3
  152.6 7.7 %fusion.13 = f32[40,2,4,1,1792]{4,0,1,2,3:T(8,128)S(1)} fusion(bf16[4,1024,1792]{2,1,0:T(8,128)(2,1)} %param.14, bf16[40,2,4,1024]{3,0,2,1:T(8,128)(2,1)S(1)} %bitcast.116), kind=kOutput, calls=%fused_computation.19 | convolution fusion | flops 1174405120 | bytes 17629184 | tf_op jit(solution)/shard_map/cnld,ldf->cnlf/dot_general | solution.py:79
  160.4 9.1 %fusion.16 = f32[40,2,4,1,1792]{4,0,1,2,3:T(8,128)} fusion(bf16[4,1024,1792]{2,1,0:T(8,128)(2,1)} %param.13, bf16[40,2,4,1024]{3,0,2,1:T(8,128)(2,1)S(1)} %bitcast.117), kind=kOutput, calls=%fused_computation.20 | convolution fusion | flops 1174405120 | bytes 17629184 | tf_op jit(solution)/shard_map/cnld,ldf->cnlf/dot_general | solution.py:78
  169.5 10.1 %fusion.19 = f32[40,2,4,1,1792]{4,0,1,2,3:T(8,128)S(1)} fusion(bf16[4,1792,1024]{2,1,0:T(8,128)(2,1)} %param.15, bf16[40,2,4,1024]{3,0,2,1:T(8,128)(2,1)} %bitcast.21), kind=kOutput, calls=%fused_computation.21 | convolution fusion | flops 1174405120 | bytes 17629184 | tf_op jit(solution)/shard_map/cnld,lfd->cnlf/dot_general | solution.py:80
  179.6 3.5 pad_maximum_fusion
  183.1 244.0 %all-reduce.2.cloned.1.call-done = f32[40,2,4,3,1792]{4,0,1,2,3:T(8,128)} async-done(((f32[40,2,4,3,1792]{4,0,1,2,3:T(8,128)}), f32[40,2,4,3,1792]{4,0,1,2,3:T(8,128)}) %all-reduce.2.cloned.1.call-update) | async-done | bytes 6881296 | tf_op jit(solution)/shard_map/psum | solution.py:83
  427.2 4.2 multiply_convert_fusion.1
  431.3 9.7 %fusion.2 = f32[4,40,2,1024]{3,1,2,0:T(8,128)S(1)} fusion(bf16[40,2,4,1792]{3,0,1,2:T(8,128)(2,1)S(1)} %get-tuple-element.5, bf16[4,1024,1792]{2,1,0:T(8,128)(2,1)} %param.13), kind=kOutput, calls=%fused_computation.5 | convolution fusion | flops 1174405120 | bytes 17137664 | tf_op jit(solution)/shard_map/cnlf,ldf->cnld/dot_general | solution.py:96
  441.0 9.9 %fusion.26 = f32[40,2,4,1024]{3,0,1,2:T(8,128)S(1)} fusion(f32[4,40,2,1024]{3,1,2,0:T(8,128)S(1)} %fusion.2, bf16[40,2,4,1792]{3,0,1,2:T(8,128)(2,1)S(1)} %get-tuple-element.4, bf16[4,1024,1792]{2,1,0:T(8,128)(2,1)} %param.14), kind=kOutput, calls=%fused_computation.31 | convolution fusion | flops 1174732800 | bytes 18448384 | tf_op jit(solution)/shard_map/cnlf,ldf->cnld/dot_general | solution.py:97
  451.8 33.9 %all_to_all.69 = f32[40,8,1024]{2,1,0:T(8,128)S(1)} all-to-all(f32[40,8,1024]{2,1,0:T(8,128)S(1)} %copy.84), channel_id=1, replica_groups=mesh['dp'=4,'expert'=2,'tensor'=4] {'dp'}, dimensions={0} | all-to-all | bytes 2621440 | tf_op jit(solution)/shard_map/all_to_all | solution.py:102
  485.7 1.9 copy.97
  487.6 3.0 reshape.40
  490.6 4.8 all-to-all-start.5
  495.5 12.0 %bitcast_convert_fusion = bf16[4,1792,1024]{2,1,0:T(8,128)(2,1)} fusion(f32[40,2,4,3,1792]{4,0,1,2,3:T(8,128)} %all-reduce.2.cloned.1.call-done, bf16[40,2,4,1024]{3,0,2,1:T(8,128)(2,1)} %bitcast.21), kind=kOutput, calls=%fused_computation | convolution fusion | flops 1185185792 | bytes 19922944 | tf_op jit(solution)/shard_map/cnlf,cnld->lfd/dot_general | solution.py:87
  507.5 12.5 %all-to-all-done.5 = f32[10,8,4096]{2,0,1:T(8,128)} async-done(((f32[10,8,4096]{2,0,1:T(8,128)}), f32[10,8,4096]{2,0,1:T(8,128)}, u32[]{:S(2)}, u32[]{:S(2)}) %all-to-all-start.5) | async-done | bytes 1310752 | tf_op jit(solution)/shard_map/all_to_all | solution.py:101
  519.9 3.7 fusion.29
  523.6 7.6 %bitcast_convert_fusion.1 = bf16[4,1024,1792]{2,1,0:T(8,128)(2,1)} fusion(bf16[40,2,4,1024]{3,0,2,1:T(8,128)(2,1)S(1)} %bitcast.118, bf16[40,2,4,1792]{3,0,1,2:T(8,128)(2,1)S(1)} %get-tuple-element.4), kind=kOutput, calls=%fused_computation.1 | convolution fusion | flops 1181745152 | bytes 16482304 | tf_op jit(solution)/shard_map/cnld,cnlf->ldf/dot_general | solution.py:93
  531.2 7.6 %bitcast_convert_fusion.2 = bf16[4,1024,1792]{2,1,0:T(8,128)(2,1)} fusion(bf16[40,2,4,1024]{3,0,2,1:T(8,128)(2,1)S(1)} %bitcast.119, bf16[40,2,4,1792]{3,0,1,2:T(8,128)(2,1)S(1)} %get-tuple-element.5), kind=kOutput, calls=%fused_computation.2 | convolution fusion | flops 1181745152 | bytes 16482304 | tf_op jit(solution)/shard_map/cnld,cnlf->ldf/dot_general | solution.py:90
  538.8 5.0 reduce-scatter.2.cloned.1.call-done
  (27 shorter events, 7.3 us)
Async XLA Ops:
  23.1 23.1 %copy-start.1 = (bf16[8,4096]{1,0:T(8,128)(2,1)S(1)}, bf16[8,4096]{1,0:T(8,128)(2,1)}, u32[]{:S(2)}) copy-start(bf16[8,4096]{1,0:T(8,128)(2,1)} %param.9) | copy-start | bytes 196612
  23.1 28.8 %copy-start.2 = (f32[32,2]{0,1:T(2,128)S(1)}, f32[32,2]{0,1:T(2,128)}, u32[]{:S(2)}) copy-start(f32[32,2]{0,1:T(2,128)} %param.10) | copy-start | bytes 772
  41.3 37.1 %all-to-all-start = ((bf16[4,2,40960]{2,1,0:T(2,128)(2,1)}), bf16[4,2,40960]{2,1,0:T(2,128)(2,1)S(1)}, u32[]{:S(2)}, u32[]{:S(2)}) async-start(bf16[4,2,40960]{2,1,0:T(2,128)(2,1)} %reshape.43), calls=%async_computation | async-start | bytes 1310720 | tf_op jit(solution)/shard_map/all_to_all | solution.py:46
  78.4 35.9 %all-to-all-start.2 = ((bf16[4,2,40960]{2,1,0:T(2,128)(2,1)}), bf16[4,2,40960]{2,1,0:T(2,128)(2,1)S(1)}, u32[]{:S(2)}, u32[]{:S(2)}) async-start(bf16[4,2,40960]{2,1,0:T(2,128)(2,1)} %reshape.41), calls=%async_computation.2 | async-start | bytes 1310720 | tf_op jit(solution)/shard_map/all_to_all | solution.py:59
  114.3 33.8 %all-to-all-start.1 = ((bf16[40,8,1024]{2,0,1:T(8,128)(2,1)}), bf16[40,8,1024]{2,0,1:T(8,128)(2,1)S(1)}, u32[]{:S(2)}, u32[]{:S(2)}) async-start(bf16[40,8,1024]{2,0,1:T(8,128)(2,1)} %copy.75), calls=%async_computation.1 | async-start | bytes 1310720 | tf_op jit(solution)/shard_map/all_to_all | solution.py:45
  148.1 21.4 %all-to-all-start.3 = ((bf16[40,8,1024]{2,0,1:T(8,128)(2,1)}), bf16[40,8,1024]{2,0,1:T(8,128)(2,1)}, u32[]{:S(2)}, u32[]{:S(2)}) async-start(bf16[40,8,1024]{2,0,1:T(8,128)(2,1)} %copy.81), calls=%async_computation.3 | async-start | bytes 1310720 | tf_op jit(solution)/shard_map/all_to_all | solution.py:58
  152.4 274.8 %all-reduce.2.cloned.1.call-start = ((), (), s32[]{:S(2)}) async-start(), calls=%async_computation.7 | async-start | bytes 13762560 | tf_op jit(solution)/shard_map/psum | solution.py:83
  169.5 10.1 %copy-start = (f32[40,2,4,1,1792]{4,0,1,2,3:T(8,128)S(1)}, f32[40,2,4,1,1792]{4,0,1,2,3:T(8,128)}, u32[]{:S(2)}) copy-start(f32[40,2,4,1,1792]{4,0,1,2,3:T(8,128)} %fusion.16) | copy-start | bytes 6881284
  490.6 29.3 %all-to-all-start.5 = ((f32[10,8,4096]{2,0,1:T(8,128)}), f32[10,8,4096]{2,0,1:T(8,128)}, u32[]{:S(2)}, u32[]{:S(2)}) async-start(f32[10,8,4096]{2,0,1:T(8,128)} %reshape.40), calls=%async_computation.5 | async-start | bytes 4194304 | tf_op jit(solution)/shard_map/all_to_all | solution.py:101
  495.4 48.3 %reduce-scatter.2.cloned.1.call-start = ((), (), s32[]{:S(2)}) async-start(), calls=%async_computation.8 | async-start | bytes 655360 | tf_op jit(solution)/shard_map/reduce_scatter | solution.py:120
Sparse Core Ops, SparseCore 0:
  183.2 243.8 all-reduce.1
  523.7 20.0 reduce-scatter.1
where the time goes:
time: 561 us; the launch traced here: 553 us
  waiting for transfers between devices  262 us (47%)
  local copies, waits for them, and re-layouts  118 us (21%)
  matrix products  78.4 us (14%)
  blocking collectives  47.1 us (8%)
  starting transfers between devices  23.3 us (4%)
  between operations  14.5 us (3%)
  other arithmetic  9.94 us (2%)
    psum x1, waiting for transfers between devices, shards(): lax.psum(jnp.stack([pre_gate, pre_up, grad_hidden], 3), 'dp')  244 us
    unnamed x10, local copies, waits for them, and re-layouts  76 us
    all_to_all x1, blocking collectives, shards(): lax.all_to_all(row_grad.reshape(rows_all, EXPERTS, slice_width), 'dp', sp...  33.9 us
    all_to_all x1, waiting for transfers between devices, shards(): lax.all_to_all(lax.all_to_all(row_grad.reshape(rows_all, EXPERTS, slice_w...  12.5 us
    dot_general x1, matrix products, shards(): jnp.einsum('cnlf,cnld->lfd', hidden, grad_rows, preferred_element_type=jn...  12 us
  transfers between devices with their start and end apart: 7, of which 3 were waited for; matrix products, arithmetic and copies ran while one was open for 24% of the time, Pallas kernels for 0%

commit v1 on v0

v1 whole, which is shorter than its diff:
```python
import functools

import jax
import jax.numpy as jnp
from jax import lax
from jax.experimental import pallas as pl
from jax.experimental.pallas import tpu as pltpu
from jax.sharding import PartitionSpec as P

EXPERTS = 8
TOP = 2
BF = jnp.bfloat16
F32 = jnp.float32


def swiglu_back(pre_gate, pre_up, grad_hidden):
    sigmoid_gate = jax.nn.sigmoid(pre_gate)
    silu_gate = pre_gate * sigmoid_gate
    hidden = (silu_gate * pre_up).astype(BF)
    up_delta = (grad_hidden * silu_gate).astype(BF)
    gate_delta = (
        grad_hidden * pre_up * sigmoid_gate * (1.0 + pre_gate * (1.0 - sigmoid_gate))
    ).astype(BF)
    return (hidden, gate_delta, up_delta)


def dot(spec, a, b):
    return jnp.einsum(spec, a, b, preferred_element_type=F32)


def ring_kernel(n, gate, up, down, hidden, gate_delta, up_delta, land, *sems):
    sum_send, sum_recv, out_send, out_recv = sems
    me = lax.axis_index("dp")
    right, left = lax.rem(me + 1, n), lax.rem(me + n - 1, n)
    parts, outs = (gate, up, down), (hidden, gate_delta, up_delta)
    rows, width = gate.shape[1:]
    cut = width // 256 * 128
    columns = (pl.ds(0, cut), pl.ds(cut, width - cut))
    to = (right, left)
    step_rows = 16
    every = [(d, m) for m in range(3) for d in range(2)]

    def chunk(d, back):
        return lax.rem(me + 2 * n - back, n) if d == 0 else lax.rem(me + back, n)

    def sum_copy(s, d, m):
        if s == 0:
            src = parts[m].at[chunk(d, 1), :, columns[d]]
        else:
            src = land.at[s - 1, m, :, columns[d]]
        return pltpu.make_async_remote_copy(
            src_ref=src,
            dst_ref=land.at[s, m, :, columns[d]],
            send_sem=sum_send.at[s, d, m],
            recv_sem=sum_recv.at[s, d, m],
            device_id={"dp": to[d]},
            device_id_type=pl.DeviceIdType.MESH,
        )

    def out_copy(s, d, m):
        piece = outs[m].at[chunk(d, s), :, columns[d]]
        return pltpu.make_async_remote_copy(
            src_ref=piece,
            dst_ref=piece,
            send_sem=out_send.at[s, d, m],
            recv_sem=out_recv.at[s, d, m],
            device_id={"dp": to[d]},
            device_id_type=pl.DeviceIdType.MESH,
        )

    barrier = pltpu.get_barrier_semaphore()
    for other in to:
        pl.semaphore_signal(
            barrier, inc=1, device_id={"dp": other}, device_id_type=pl.DeviceIdType.MESH
        )
    pl.semaphore_wait(barrier, 2)

    for d, m in every:
        sum_copy(0, d, m).start()
    for s in range(n - 2):
        for d, m in every:
            sum_copy(s, d, m).wait_recv()
            at = chunk(d, s + 2)

            @pl.loop(0, rows // step_rows)
            def _(i):
                r = pl.ds(pl.multiple_of(i * step_rows, step_rows), step_rows)
                own = parts[m][at, r, columns[d]].astype(F32)
                land[s, m, r, columns[d]] = (
                    land[s, m, r, columns[d]].astype(F32) + own
                ).astype(BF)

            sum_copy(s + 1, d, m).start()
    for d in range(2):
        for m in range(3):
            sum_copy(n - 2, d, m).wait_recv()

        @pl.loop(0, rows // step_rows)
        def _(i):
            r = pl.ds(pl.multiple_of(i * step_rows, step_rows), step_rows)
            values = [
                land[n - 2, m, r, columns[d]].astype(F32)
                + parts[m][me, r, columns[d]].astype(F32)
                for m in range(3)
            ]
            for ref, value in zip(outs, swiglu_back(*values)):
                ref[me, r, columns[d]] = value

        for m in range(3):
            out_copy(0, d, m).start()
    for s in range(n - 1):
        for d, m in every:
            out_copy(s, d, m).wait_recv()
            if s < n - 2:
                out_copy(s + 1, d, m).start()
    for s in range(n - 1):
        for d, m in every:
            sum_copy(s, d, m).wait_send()
            out_copy(s, d, m).wait_send()


def ring_back(pre_gate, pre_up, grad_hidden):
    n = lax.axis_size("dp")
    rows, width = pre_gate.shape[0] // n, pre_gate.shape[1]
    shape = jax.ShapeDtypeStruct((n, rows, width), BF)
    spec = pl.BlockSpec(memory_space=pltpu.VMEM)
    sems = pltpu.SemaphoreType.DMA((n - 1, 2, 3))
    return pl.pallas_call(
        functools.partial(ring_kernel, n),
        out_shape=[shape] * 3,
        in_specs=[spec] * 3,
        out_specs=[spec] * 3,
        scratch_shapes=[pltpu.VMEM((n - 1, 3, rows, width), BF), sems, sems, sems, sems],
        compiler_params=pltpu.CompilerParams(
            collective_id=0, has_side_effects=True, vmem_limit_bytes=40 * 2**20
        ),
    )(*[v.reshape(n, rows, width) for v in (pre_gate, pre_up, grad_hidden)])


def shards(tokens, out_grad, route_probs, expert_ids, slot_index, w_gate, w_up, w_down):
    n_dp, n_ex, n_tn = lax.axis_size("dp"), lax.axis_size("expert"), lax.axis_size("tensor")
    rows, width = tokens.shape
    piece = width // n_dp
    block_rows = rows * n_tn
    blocks = n_dp * n_ex
    everyone = blocks * block_rows
    capacity = 5 * block_rows * TOP // (4 * EXPERTS)
    local_experts = w_gate.shape[0]
    hidden_width = w_gate.shape[2]
    slots = blocks * capacity

    both = jnp.concatenate([tokens, out_grad], 0)
    both = both.reshape(2 * rows, n_dp, piece).transpose(1, 0, 2)
    both = lax.all_to_all(both, "dp", split_axis=0, concat_axis=0, tiled=True)
    both = lax.all_gather(both, ("expert", "tensor"), axis=0, tiled=False)
    x_all = both[:, :, :rows].reshape(everyone, piece)
    g_all = both[:, :, rows:].reshape(everyone, piece)

    routes = jnp.concatenate(
        [expert_ids.astype(F32), slot_index.astype(F32), route_probs], axis=1
    )
    routes = lax.all_gather(routes, ("dp", "expert"), axis=0, tiled=True)
    routes = routes.reshape(n_dp, n_ex, n_tn, rows, 3 * TOP)
    routes = routes.transpose(4, 1, 2, 0, 3).reshape(3 * TOP, everyone)
    ids = routes[:TOP].astype(jnp.int32)
    slot = routes[TOP : 2 * TOP].astype(jnp.int32)
    probs = routes[2 * TOP :]
    at = jnp.arange(everyone, dtype=jnp.int32)
    block = (at // rows) % n_dp * n_ex + at // (rows * n_dp * n_tn)
    mine = ids - lax.axis_index("expert") * local_experts
    kept = (slot < capacity) & (mine >= 0) & (mine < local_experts)
    target = jnp.where(kept, mine * slots + block[None] * capacity + slot, -1)
    places = jnp.arange(local_experts * slots, dtype=jnp.int32)
    hits = [places[:, None] == target[k][None] for k in range(TOP)]
    table = sum(h.astype(F32) for h in hits).astype(BF)
    slot_prob = sum(
        jnp.sum(jnp.where(hits[k], probs[k][None], 0.0), axis=1) for k in range(TOP)
    )
    token_rows = dot("st,td->sd", table, x_all).astype(BF)
    grad_rows = (dot("st,td->sd", table, g_all) * slot_prob[:, None]).astype(BF)
    token_rows = token_rows.reshape(local_experts, slots, piece)
    grad_rows = grad_rows.reshape(local_experts, slots, piece)

    def flat(value):
        return value.astype(BF).reshape(local_experts * slots, hidden_width)

    together = ring_back(
        flat(dot("lsd,ldf->lsf", token_rows, w_gate)),
        flat(dot("lsd,ldf->lsf", token_rows, w_up)),
        flat(dot("lsd,lfd->lsf", grad_rows, w_down)),
    )
    hidden, gate_delta, up_delta = [
        v.reshape(local_experts, slots, hidden_width) for v in together
    ]

    row_grad = dot("lsf,ldf->lsd", gate_delta, w_gate) + dot("lsf,ldf->lsd", up_delta, w_up)
    row_grad = row_grad.astype(BF).reshape(local_experts * slots, piece)
    token_part = dot("st,sd->td", table, row_grad).astype(BF)
    token_grad = lax.psum_scatter(
        token_part, ("expert", "tensor"), scatter_dimension=0, tiled=True
    )
    token_grad = token_grad.reshape(n_dp, rows, piece)
    token_grad = lax.all_to_all(token_grad, "dp", split_axis=0, concat_axis=0, tiled=True)
    token_grad = token_grad.transpose(1, 0, 2).reshape(rows, width)

    grad_gate = dot("lsd,lsf->ldf", token_rows, gate_delta).astype(BF)
    grad_up = dot("lsd,lsf->ldf", token_rows, up_delta).astype(BF)
    grad_down = dot("lsf,lsd->lfd", hidden, grad_rows).astype(BF)
    return (token_grad, grad_gate, grad_up, grad_down)


def solution(mesh):
    placed = (
        P(("dp", "expert", "tensor"), None),
        P(("dp", "expert", "tensor"), None),
        P(("dp", "expert"), None),
        P(("dp", "expert"), None),
        P(("dp", "expert"), None),
        P("expert", "dp", "tensor"),
        P("expert", "dp", "tensor"),
        P("expert", "tensor", "dp"),
    )
    return jax.shard_map(
        shards,
        mesh=mesh,
        in_specs=placed,
        out_specs=(
            P(("dp", "expert", "tensor"), None),
            P("expert", "dp", "tensor"),
            P("expert", "dp", "tensor"),
            P("expert", "tensor", "dp"),
        ),
        check_vma=False,
    )
```

time: 561 us -> 262 us (0.47); the launches traced: 553 us -> 261 us
  waiting for transfers between devices: 262 us -> 19.2 us
  local copies, waits for them, and re-layouts: 118 us -> 4.36 us
  Pallas kernels: 0 us -> 107 us
  starting transfers between devices: 23.3 us -> 4.65 us
  matrix products: 78.4 us -> 65.7 us
  other arithmetic: 9.94 us -> 3.19 us
    psum x1 -> x0, waiting for transfers between devices: 244 us -> none  [shards(): lax.psum(jnp.stack([pre_gate, pre_up, grad_hidden], 3), 'dp')]
    pallas_call x0 -> x1, Pallas kernels: none -> 107 us  [ring_back(): pl.pallas_call(functools.partial(ring_kernel, n), out_shape=[shape] * 3,...]
    unnamed x10 -> x11, local copies, waits for them, and re-layouts: 76 us -> 2.22 us
    all_to_all x8 -> x0, local copies, waits for them, and re-layouts: 25.9 us -> none  [the longest x3 10.5 us: shards(): lax.all_to_all(x_buf.reshape(capacity, EXPERTS, model_width), 'dp', split...]
    all_to_all x1, blocking collectives: 33.9 us -> 12.3 us  [shards(): both = lax.all_to_all(both, 'dp', split_axis=0, concat_axis=0, tiled=True)]
    all_to_all x5 -> x1, starting transfers between devices: 23 us -> 4.57 us  [shards(): lax.all_to_all(token_grad, 'dp', split_axis=0, concat_axis=0, tiled=True)]
    all_gather x2 -> x1, blocking collectives: 13.2 us -> 30.6 us  [shards(): routes = lax.all_gather(routes, ('dp', 'expert'), axis=0, tiled=True)]
    reshape x3 -> x2, local copies, waits for them, and re-layouts: 15.7 us -> 0.18 us  [the longest x1 0.1 us: shards(): routes = routes.reshape(n_dp, n_ex, n_tn, rows, 3 * TOP)]
  transfers between devices with their start and end apart: 7 -> 3, of which waited for: 3 -> 1; matrix products, arithmetic and copies ran while one was open for 24% -> 10% of each run, Pallas kernels for 0% -> 0%
where the time goes in v1:
time: 262 us; the launch traced here: 261 us
  Pallas kernels  107 us (41%)
  matrix products  65.7 us (25%)
  blocking collectives  42.9 us (16%)
  waiting for transfers between devices  19.2 us (7%)
  between operations  14.3 us (5%)
  starting transfers between devices  4.65 us (2%)
  local copies, waits for them, and re-layouts  4.36 us (2%)
  other arithmetic  3.19 us (1%)
    pallas_call x1, Pallas kernels, ring_back(): pl.pallas_call(functools.partial(ring_kernel, n), out_shape=[shape] * 3,...  107 us
    dot_general x11, matrix products, dot(): return jnp.einsum(spec, a, b, preferred_element_type=F32)  65.7 us
    all_gather x1, blocking collectives, shards(): routes = lax.all_gather(routes, ('dp', 'expert'), axis=0, tiled=True)  30.6 us
    reduce_scatter x1, waiting for transfers between devices, shards(): lax.psum_scatter(token_part, ('expert', 'tensor'), scatter_dimension=0, t...  19.1 us
    all_to_all x1, blocking collectives, shards(): both = lax.all_to_all(both, 'dp', split_axis=0, concat_axis=0, tiled=True)  12.3 us
  transfers between devices with their start and end apart: 3, of which 1 were waited for; matrix products, arithmetic and copies ran while one was open for 10% of the time, Pallas kernels for 0%

profile of v1, /device:TPU:0, one launch (start us, length us, event | category | flops | bytes accessed | tf_op | source)
XLA Modules:
  0.0 261.1 jit_solution(1369800989589262918)
XLA Ops:
  7.2 0.9 pad_maximum_fusion
  8.1 0.1 reshape.95
  8.2 12.3 %all_to_all.10 = bf16[4,16,1024]{2,1,0:T(8,128)(2,1)} all-to-all(bf16[4,16,1024]{2,1,0:T(8,128)(2,1)S(1)} %copy.48), channel_id=1, replica_groups=mesh['dp'=4,'expert'=2,'tensor'=4] {'dp'}, dimensions={0} | all-to-all | bytes 262144 | tf_op jit(solution)/shard_map/all_to_all | solution.py:154
  20.6 0.7 convert_element_type.55
  21.3 0.7 convert_element_type.56
  22.0 0.7 maximum_bitcast_fusion
  22.7 30.6 %all-gather.1 = f32[8,32,6]{1,2,0:T(8,128)S(1)} all-gather(f32[1,32,6]{1,2,0:T(8,128)S(1)} %maximum_bitcast_fusion), channel_id=1, replica_groups=mesh['dp'=4,'expert'=2,'tensor'=4] {'dp','expert'}, dimensions={0}, use_global_device_ids=true | all-gather | bytes 6912 | tf_op jit(solution)/shard_map/all_gather | solution.py:162
  53.3 0.1 reshape.94
  53.5 0.1 ge.11
  53.6 0.1 lt.25
  53.7 0.1 mul.44
  53.8 0.1 broadcast_in_dim.34
  54.0 0.1 convert_element_type.58
  54.1 0.1 broadcast_in_dim.31
  54.2 0.2 select_reduce_fusion
  54.4 1.3 fusion.16
  55.7 0.3 convolution_convert_fusion.6
  56.1 8.0 %convolution_convert_fusion.4.up = bf16[4,80,1792]{2,1,0:T(8,128)(2,1)S(1)} fusion(bf16[4,80,1024]{2,1,0:T(8,128)(2,1)S(1)} %bitcast.37, bf16[4,1024,1792]{2,1,0:T(8,128)(2,1)} %param.14), kind=kOutput, calls=%fused_computation.4 | convolution fusion | flops 1174978560 | bytes 16482304 | tf_op jit(solution)/shard_map/lsd,ldf->lsf/dot_general | solution.py:28
  64.1 1.6 copy-done
  65.7 2.5 convolution_convert_fusion.5.gate
  68.2 0.4 fusion.1
  68.6 10.0 %convolution_convert_fusion.3.down = bf16[4,80,1792]{2,1,0:T(8,128)(2,1)S(1)} fusion(bf16[4,80,1024]{2,1,0:T(8,128)(2,1)S(1)} %bitcast.41, bf16[4,1792,1024]{2,1,0:T(8,128)(2,1)} %param.15), kind=kOutput, calls=%fused_computation.3 | convolution fusion | flops 1174978560 | bytes 16482304 | tf_op jit(solution)/shard_map/lsd,lfd->lsf/dot_general | solution.py:28
  78.5 106.8 %shard_map.111 = (bf16[4,80,1792]{2,1,0:T(8,128)(2,1)S(1)}, bf16[4,80,1792]{2,1,0:T(8,128)(2,1)S(1)}, bf16[4,80,1792]{2,1,0:T(8,128)(2,1)S(1)}) custom-call(bf16[4,80,1792]{2,1,0:T(8,128)(2,1)S(1)} %convolution_convert_fusion.5.gate, bf16[4,80,1792]{2,1,0:T(8,128)(2,1)S(1)} %convolution_convert_fusion.4.up, ...), custom_call_target="tpu_custom_call" | custom-call | tf_op jit(solution)/shard_map/pallas_call | solution.py:128
  185.3 9.7 %fusion.19 = f32[4,80,1024]{2,1,0:T(8,128)S(1)} fusion(bf16[4,80,1792]{2,1,0:T(8,128)(2,1)S(1)} %get-tuple-element.7, bf16[4,1024,1792]{2,1,0:T(8,128)(2,1)} %param.13), kind=kOutput, calls=%fused_computation.49 | convolution fusion | flops 1174405120 | bytes 17137664 | tf_op jit(solution)/shard_map/lsf,ldf->lsd/dot_general | solution.py:28
  195.0 9.7 %fusion = bf16[4,80,1024]{2,1,0:T(8,128)(2,1)S(1)} fusion(f32[4,80,1024]{2,1,0:T(8,128)S(1)} %fusion.19, bf16[4,80,1792]{2,1,0:T(8,128)(2,1)S(1)} %get-tuple-element.8, bf16[4,1024,1792]{2,1,0:T(8,128)(2,1)} %param.14), kind=kOutput, calls=%fused_computation.8 | convolution fusion | flops 1175060480 | bytes 17793024 | tf_op jit(solution)/shard_map/lsf,ldf->lsd/dot_general | solution.py:28
  204.7 1.3 convolution_convert_fusion.7
  206.0 8.7 %convolution_convert_fusion.1 = bf16[4,1024,1792]{2,1,0:T(8,128)(2,1)} fusion(bf16[4,80,1024]{2,1,0:T(8,128)(2,1)} %bitcast.39, bf16[4,80,1792]{2,1,0:T(8,128)(2,1)S(1)} %get-tuple-element.8), kind=kOutput, calls=%fused_computation.1 | convolution fusion | flops 1181745152 | bytes 16482304 | tf_op jit(solution)/shard_map/lsd,lsf->ldf/dot_general | solution.py:28
  214.7 7.6 %convolution_convert_fusion.2 = bf16[4,1024,1792]{2,1,0:T(8,128)(2,1)} fusion(bf16[4,80,1024]{2,1,0:T(8,128)(2,1)S(1)} %bitcast.40, bf16[4,80,1792]{2,1,0:T(8,128)(2,1)S(1)} %get-tuple-element.7), kind=kOutput, calls=%fused_computation.2 | convolution fusion | flops 1181745152 | bytes 16482304 | tf_op jit(solution)/shard_map/lsd,lsf->ldf/dot_general | solution.py:28
  222.3 19.1 %reduce-scatter.2.cloned.1.call-done = bf16[32,1024]{1,0:T(8,128)(2,1)} async-done(((bf16[256,1024]{1,0:T(8,128)(2,1)}), bf16[32,1024]{1,0:T(8,128)(2,1)}) %reduce-scatter.2.cloned.1.call-update) | async-done | bytes 65552 | tf_op jit(solution)/shard_map/reduce_scatter | solution.py:199
  241.5 4.6 %all-to-all-start.1 = ((bf16[4,8,1024]{2,1,0:T(8,128)(2,1)}), bf16[4,8,1024]{2,1,0:T(8,128)(2,1)S(1)}, u32[]{:S(2)}, u32[]{:S(2)}) async-start(bf16[4,8,1024]{2,1,0:T(8,128)(2,1)} %bitcast.53), calls=%async_computation.2 | async-start | bytes 131072 | tf_op jit(solution)/shard_map/all_to_all | solution.py:203
  246.0 7.6 %convolution_convert_fusion = bf16[4,1792,1024]{2,1,0:T(8,128)(2,1)} fusion(bf16[4,80,1792]{2,1,0:T(8,128)(2,1)S(1)} %get-tuple-element.9, bf16[4,80,1024]{2,1,0:T(8,128)(2,1)S(1)} %bitcast.42), kind=kOutput, calls=%fused_computation | convolution fusion | flops 1181745152 | bytes 16482304 | tf_op jit(solution)/shard_map/lsf,lsd->lfd/dot_general | solution.py:28
  253.6 0.6 copy.52
  (31 shorter events, 0.4 us)
Async XLA Ops:
  7.2 47.3 %all-gather.4.cloned.1.call-start = ((), (), s32[]{:S(2)}) async-start(), calls=%async_computation.4 | async-start | bytes 1179648 | tf_op jit(solution)/shard_map/all_gather | solution.py:155
  20.6 220.9 %reduce-scatter.2.cloned.1.call-start = ((), (), s32[]{:S(2)}) async-start(), calls=%async_computation.3 | async-start | bytes 589824 | tf_op jit(solution)/shard_map/reduce_scatter | solution.py:199
  56.1 8.0 %copy-start.1 = (bf16[320,1024]{1,0:T(8,128)(2,1)}, bf16[320,1024]{1,0:T(8,128)(2,1)S(1)}, u32[]{:S(2)}) copy-start(bf16[320,1024]{1,0:T(8,128)(2,1)S(1)} %convolution_convert_fusion.6) | copy-start | bytes 1966084
  56.1 9.6 %copy-start = (bf16[4,1024,1792]{2,1,0:T(8,128)(2,1)S(1)}, bf16[4,1024,1792]{2,1,0:T(8,128)(2,1)}, u32[]{:S(2)}) copy-start(bf16[4,1024,1792]{2,1,0:T(8,128)(2,1)} %param.13) | copy-start | bytes 44040196
  68.6 10.0 %copy-start.3 = (bf16[320,1024]{1,0:T(8,128)(2,1)}, bf16[320,1024]{1,0:T(8,128)(2,1)S(1)}, u32[]{:S(2)}) copy-start(bf16[320,1024]{1,0:T(8,128)(2,1)S(1)} %fusion.1) | copy-start | bytes 1966084
  206.0 8.7 %copy-start.2 = (bf16[320,1024]{1,0:T(8,128)(2,1)S(1)}, bf16[320,1024]{1,0:T(8,128)(2,1)}, u32[]{:S(2)}) copy-start(bf16[320,1024]{1,0:T(8,128)(2,1)} %copy-done.1) | copy-start | bytes 1966084
  214.7 31.3 %copy-start.4 = (bf16[320,1024]{1,0:T(8,128)(2,1)S(1)}, bf16[320,1024]{1,0:T(8,128)(2,1)}, u32[]{:S(2)}) copy-start(bf16[320,1024]{1,0:T(8,128)(2,1)} %copy-done.3) | copy-start | bytes 1966084
  241.5 12.2 %all-to-all-start.1 = ((bf16[4,8,1024]{2,1,0:T(8,128)(2,1)}), bf16[4,8,1024]{2,1,0:T(8,128)(2,1)S(1)}, u32[]{:S(2)}, u32[]{:S(2)}) async-start(bf16[4,8,1024]{2,1,0:T(8,128)(2,1)} %bitcast.53), calls=%async_computation.2 | async-start | bytes 131072 | tf_op jit(solution)/shard_map/all_to_all | solution.py:203
Sparse Core Ops, SparseCore 0:
  20.7 22.4 all-gather.3
  206.1 35.2 reduce-scatter.1
